TPU v7x, 256 devices: a whole 4x4x8 slice. The times are simulated.
256 devices in a mesh: coil: 8 (over y, core), spoke: 32 (over x, z).
Axes of the slice: x: 4, y: 4, z: 8, core: 2. Of those that a mesh axis runs over, the one named last changes fastest.
Arguments:
- kdata: bfloat16 [256, 16, 2, 64, 256], P('spoke', 'coil'), may hold values from -6 to 6
- coords: float32 [256, 2, 256], P('spoke'), may hold values from 0 to 256, as said below
- foot_offset: int32 [256, 32], P('spoke'), may hold values from 0 to 224, as said below
- live_count: int32 [32], P('spoke'), may hold values from 1 to 8, 192 in all
- dcf_table: float32 [129], replicated, may hold values from 0.1 to 4
- dcf_index: int32 [256, 256], P('spoke'), may hold values from 0 to 128
- slab_owner: int32 [32], replicated, may hold values from 0 to 31, each once
Outputs:
- coil_images: float32 [256, 16, 2, 64, 256], P('spoke', 'coil')
- combined: float32 [256, 64, 256], P('spoke', 'coil')
Inputs may be any that keep to these rules, and one draw needn't show every extreme that they name: coords[p, 0, s] lies between s and s + 1; coords[p, 1, s] lies between foot_offset[p, s // 8] + 3 and foot_offset[p, s // 8] + 29. `foot_offset`: for each block of 8 spoke slots (the slots of one device index of spoke) and each slab, the offsets lie between b and b + 16, where b is the smallest of them, and both ends are taken; b <= 208.
All inputs are finite; a program needn't handle non-finite values. No bound on the sum of `live_count` on one device may be relied on, other than what follows from the above.
Results may differ from a plain program's by a relative error of at most 0.0028.
Values may be sent and summed in bfloat16 or wider, within the bound.
A program may use at most 128 MiB of HBM per device.

v0:
```python
import math

import jax
import jax.numpy as jnp
from jax import lax
from jax.sharding import PartitionSpec as P

FW = 32
UW = 48
HALO = 4


def cut_along(shard, dim, count):
    before, after = (shard.shape[:dim], shard.shape[dim + 1 :])
    return jnp.moveaxis(shard.reshape(*before, count, -1, *after), dim, 0)


def sent_and_summed(shard, axis, dim):
    count = lax.axis_size(axis)
    parts = lax.all_to_all(cut_along(shard, dim, count), axis, 0, 0, tiled=True)
    return jnp.sum(parts.astype(jnp.float32), axis=0)


def kernel(distance):
    inner = jnp.maximum(1.0 - distance * distance * 0.25, 0.0)
    return inner * inner


def inverse_table(length):
    counter = jnp.arange(length, dtype=jnp.int32)
    phase = (
        2.0 * math.pi / length * (counter[:, None] * counter[None, :] % length).astype(jnp.float32)
    )
    factor = 1.0 / math.sqrt(length)
    return (jnp.cos(phase) * factor, jnp.sin(phase) * factor)


def product(left, right):
    return jnp.dot(left, right, precision=lax.Precision.HIGHEST, preferred_element_type=jnp.float32)


def depth_product(left, right):
    return jnp.einsum("akg,kz->azg", left, right, precision=lax.Precision.HIGHEST)


def on_device(kdata, coords, foot_offset, live_count, dcf_table, dcf_index, slab_owner):
    slot_count, coil_dev, part_count, kz_len, grid_len = kdata.shape
    slab_count = lax.axis_size("spoke")
    slab_rows = grid_len // slab_count
    block_len = slab_rows + 2 * HALO
    columns = coil_dev * part_count * kz_len
    live_flag = (jnp.arange(slot_count, dtype=jnp.int32) < live_count[0]).astype(jnp.float32)
    table_len = dcf_table.shape[0]
    table_hit = dcf_index[:, :, None] == jnp.arange(table_len, dtype=jnp.int32)[None, None, :]
    density = (
        jnp.sum(jnp.where(table_hit, dcf_table[None, None, :], 0.0), axis=2) * live_flag[:, None]
    )
    slab_first = jnp.arange(slab_count, dtype=jnp.int32) * slab_rows
    position = (
        slab_first[:, None] - HALO + jnp.arange(block_len, dtype=jnp.int32)[None, :]
    ).reshape(-1)
    inside = ((position >= 0) & (position < grid_len)).reshape(slab_count, block_len)
    clipped = jnp.clip(position, 0, grid_len - 1)
    samples_last = jnp.transpose(kdata.reshape(slot_count, columns, grid_len), (0, 2, 1))
    blocks = jnp.take(samples_last, clipped, axis=1).reshape(
        slot_count, slab_count, block_len, columns
    )
    blocks = jnp.where(inside[None, :, :, None], blocks, jnp.zeros((), kdata.dtype))
    row_coord = jnp.take(coords[:, 0, :], clipped, axis=1).reshape(
        slot_count, slab_count, block_len
    )
    col_coord = jnp.take(coords[:, 1, :], clipped, axis=1).reshape(
        slot_count, slab_count, block_len
    )
    block_density = jnp.where(
        inside[None],
        jnp.take(density, clipped, axis=1).reshape(slot_count, slab_count, block_len),
        0.0,
    )
    device = lax.axis_index("spoke")
    owned_slab = slab_owner[device]
    start_cols = jnp.broadcast_to(
        foot_offset.astype(jnp.float32)[:, :, None], (slot_count, slab_count, block_len)
    )
    geometry = jnp.stack([row_coord, col_coord, block_density, start_cols], axis=2)
    sent_values = jnp.take(blocks, slab_owner, axis=1)
    sent_geometry = jnp.take(geometry, slab_owner, axis=1)
    got_values = lax.all_to_all(
        sent_values, "spoke", split_axis=1, concat_axis=0, tiled=True
    ).reshape(slab_count, slot_count, block_len, columns)
    got_geometry = lax.all_to_all(
        sent_geometry, "spoke", split_axis=1, concat_axis=0, tiled=True
    ).reshape(slab_count, slot_count, 4, block_len)
    row_cells = (owned_slab * slab_rows + jnp.arange(slab_rows, dtype=jnp.int32)).astype(
        jnp.float32
    )
    window_cols = jnp.arange(UW, dtype=jnp.int32)
    grid_cols = jnp.arange(grid_len, dtype=jnp.int32)
    senders = min(8, slab_count)

    def add_block(turn_index, running):
        values = lax.dynamic_slice_in_dim(got_values, turn_index * senders, senders, 0)
        geometry_part = lax.dynamic_slice_in_dim(got_geometry, turn_index * senders, senders, 0)
        sender_base = jnp.min(geometry_part[:, :, 3, 0], axis=1).astype(jnp.int32)
        cells = (sender_base[:, None] + window_cols[None, :]).astype(jnp.float32)[:, None, None, :]
        row_weight = geometry_part[:, :, 2, :, None] * kernel(
            row_cells[None, None, None, :] + 0.5 - geometry_part[:, :, 0, :, None]
        )
        start = geometry_part[:, :, 3, :, None]
        covered = (cells >= start) & (cells < start + FW)
        col_weight = jnp.where(covered, kernel(cells + 0.5 - geometry_part[:, :, 1, :, None]), 0.0)
        weights = (
            (row_weight[..., None] * col_weight[..., None, :])
            .reshape(senders, slot_count, block_len, slab_rows * UW)
            .astype(jnp.bfloat16)
        )
        windows = jnp.einsum(
            "stqc,stqk->sck", values, weights, preferred_element_type=jnp.float32
        ).reshape(senders, columns, slab_rows, UW)
        shifted = sender_base[:, None, None] + window_cols[None, :, None]
        placement = (shifted == grid_cols[None, None, :]).astype(jnp.float32)
        return running + jnp.einsum(
            "scij,sjg->cig", windows, placement, precision=lax.Precision.HIGHEST
        )

    slab_grid = lax.fori_loop(
        0, slab_count // senders, add_block, jnp.zeros((columns, slab_rows, grid_len), jnp.float32)
    )
    cosine_table, sine_table = inverse_table(grid_len)
    layered = slab_grid.reshape(coil_dev, part_count, kz_len * slab_rows, grid_len)
    real_part = layered[:, 0].reshape(-1, grid_len)
    imag_part = layered[:, 1].reshape(-1, grid_len)
    row_real = (product(real_part, cosine_table) - product(imag_part, sine_table)).reshape(
        coil_dev, kz_len, slab_rows * grid_len
    )
    row_imag = (product(real_part, sine_table) + product(imag_part, cosine_table)).reshape(
        coil_dev, kz_len, slab_rows * grid_len
    )
    depth_cosine, depth_sine = inverse_table(kz_len)
    image_real = depth_product(row_real, depth_cosine) - depth_product(row_imag, depth_sine)
    image_imag = depth_product(row_real, depth_sine) + depth_product(row_imag, depth_cosine)
    images = jnp.stack([image_real, image_imag], axis=1).reshape(
        coil_dev, part_count, kz_len, slab_rows, grid_len
    )
    power_sum = jnp.transpose(jnp.sum(images * images, axis=(0, 1)), (1, 0, 2))
    coil_images = jnp.transpose(images, (3, 0, 1, 2, 4))
    total_power = sent_and_summed(power_sum.astype(jnp.bfloat16), "coil", 1)
    combined = jnp.sqrt(total_power)
    return (coil_images, combined)


def solution(mesh):
    return jax.shard_map(
        on_device,
        mesh=mesh,
        in_specs=(
            P("spoke", "coil", None, None, None),
            P("spoke", None, None),
            P("spoke", None),
            P("spoke"),
            P(),
            P("spoke", None),
            P(),
        ),
        out_specs=(P("spoke", "coil", None, None, None), P("spoke", "coil", None)),
        check_vma=False,
    )
```

profile of v0, /device:TPU:1, one launch (start us, length us, event | category | flops | bytes accessed | tf_op | source)
XLA Modules:
  0.0 172.8 jit_solution(4568289985114552830)
XLA Ops:
  0.6 0.7 compare_and_fusion.2
  1.3 0.7 compare_select_fusion.3
  2.9 0.7 convert_element_type.88
  3.7 0.8 fusion.95
  4.6 0.9 select_reduce_fusion
  5.8 1.0 gather_fusion.5
  6.8 1.0 gather_fusion.3
  8.0 1.0 gather_fusion.4
  9.7 0.6 gather_fusion.2
  10.4 0.9 reshape.385
  11.3 11.9 %all-to-all-start.1 = ((f32[32,1,512]{2,1,0:T(1,128)}), f32[32,1,512]{2,1,0:T(1,128)S(1)}, u32[]{:S(2)}, u32[]{:S(2)}) async-start(f32[32,1,512]{2,1,0:T(1,128)} %reshape.385), calls=%async_computation.1 | async-start | bytes 131072 | tf_op jit(solution)/shard_map/all_to_all | solution.py:91
  23.3 1.0 copy.86
  24.3 1.7 %gather_fusion = bf16[512,8,256]{2,1,0:T(8,128)(2,1)S(1)} fusion(bf16[8,256,256]{2,0,1:T(8,128)(2,1)S(1)} %bitcast.138, s32[1024]{0:T(1024)S(1)} %pad_clamp_fusion.2), kind=kCustom, calls=%fused_computation.3 | custom fusion | bytes 4196352 | tf_op jit(solution)/shard_map/jit(_take)/gather | solution.py:65
  26.0 0.4 copy.87
  26.8 2.0 %gather_fusion.1 = bf16[32,8,16,256]{3,2,1,0:T(8,128)(2,1)} fusion(bf16[8,32,16,256]{3,2,1,0:T(8,128)(2,1)S(1)} %select_select_fusion, s32[1024]{0:T(1024)S(1)} %get-tuple-element.210), kind=kCustom, calls=%fused_computation.4 | custom fusion | bytes 4194432 | tf_op jit(solution)/shard_map/jit(_take)/gather | solution.py:86
  28.8 3.2 %select_bitcast_fusion = bf16[8,32,16,256]{3,2,0,1:T(8,128)(2,1)} fusion(bf16[32,8,16,256]{3,2,1,0:T(8,128)(2,1)} %gather_fusion.1, pred[32]{0:T(512)(128)(4,1)S(1)} %compare_and_fusion.2), kind=kLoop, calls=%fused_computation.32 | loop fusion | flops 1048576 | bytes 4194336 | tf_op jit(solution)/shard_map/jit(_take)/select_n | solution.py:86
  32.0 9.4 %all-to-all-start = ((bf16[8,32,16,256]{3,2,0,1:T(8,128)(2,1)}), bf16[8,32,16,256]{3,2,0,1:T(8,128)(2,1)S(1)}, u32[]{:S(2)}, u32[]{:S(2)}) async-start(bf16[8,32,16,256]{3,2,0,1:T(8,128)(2,1)} %select_bitcast_fusion), calls=%async_computation | async-start | bytes 4194304 | tf_op jit(solution)/shard_map/all_to_all | solution.py:88
  41.4 0.7 dynamic_slice.17
  42.7 0.6 broadcast.532
  43.3 0.8 reduce.1
  44.4 46.3 %all-to-all-done = bf16[8,32,16,256]{3,2,0,1:T(8,128)(2,1)S(1)} async-done(((bf16[8,32,16,256]{3,2,0,1:T(8,128)(2,1)}), bf16[8,32,16,256]{3,2,0,1:T(8,128)(2,1)S(1)}, u32[]{:S(2)}, u32[]{:S(2)}) %all-to-all-start) | async-done | bytes 2097184 | tf_op jit(solution)/shard_map/all_to_all | solution.py:88
  90.7 44.7 %while.14 = (s32[]{:T(128)}, f32[256,8,256]{2,0,1:T(8,128)}, bf16[32,8,16,256]{3,2,1,0:T(8,128)(2,1)S(1)}, f32[32,8,4,16]{3,1,2,0:T(8,128)S(1)}, s32[]{:T(128)},...) while((s32[]{:T(128)}, f32[256,8,256]{2,0,1:T(8,128)}, ...), condition=%wide.region_3.5_spmd.clone, body=%wide.region_1.4_spmd.clone.sunk | while | flops 2619730944 | bytes 48236364 | solution.py:126
  91.0 0.5 multiply_select_fusion.2
  91.5 0.5 copy-done
  92.4 1.3 multiply_convert_fusion.2
  93.6 1.4 convert_element_type.149
  95.1 1.8 %fusion.119 = f32[8,256,384,1]{1,2,3,0:T(8,128)S(1)} fusion(bf16[8,8,16,384]{3,2,1,0:T(8,128)(2,1)S(1)} %convert_element_type.149, bf16[32,8,16,256]{3,2,1,0:T(8,128)(2,1)} %copy-done, s32[]{:T(128)S(6)} %select_n.198), kind=kOutput, calls=%fused_computation.13.clone.1 | convolution fusion | flops 201326592 | bytes 4456452 | tf_op jit(solution)/shard_map/while/body/eval_jaxpr/stqc,stqk->sck/dot_general | solution.py:117
  96.9 3.6 %bitcast_add_fusion.2 = f32[256,8,256]{2,0,1:T(8,128)S(1)} fusion(f32[256,8,256]{2,0,1:T(8,128)S(1)} %copy-done.5, f32[8,256,8,48]{1,3,2,0:T(8,128)S(1)} %bitcast.132, pred[]{:T(512)S(6)} %compare.5, s32[8,48]{1,0:T(8,128)S(1)} %get-tuple-element.255), kind=kOutput, calls=%fused_computation.10.clone.1 | convolution fusion | flops 2417065984 | bytes 7341569 | tf_op jit(solution)/shard_map/while/body/eval_jaxpr/scij,sjg->cig/dot_general | solution.py:122
  100.5 1.3 copy-done.6
  102.2 0.5 multiply_select_fusion.2
  102.7 0.5 copy-done
  103.5 1.3 multiply_convert_fusion.2
  104.8 1.4 convert_element_type.149
  106.3 1.8 %fusion.119 = f32[8,256,384,1]{1,2,3,0:T(8,128)S(1)} fusion(bf16[8,8,16,384]{3,2,1,0:T(8,128)(2,1)S(1)} %convert_element_type.149, bf16[32,8,16,256]{3,2,1,0:T(8,128)(2,1)} %copy-done, s32[]{:T(128)S(6)} %select_n.198), kind=kOutput, calls=%fused_computation.13.clone.1 | convolution fusion | flops 201326592 | bytes 4456452 | tf_op jit(solution)/shard_map/while/body/eval_jaxpr/stqc,stqk->sck/dot_general | solution.py:117
  108.1 3.6 %bitcast_add_fusion.2 = f32[256,8,256]{2,0,1:T(8,128)S(1)} fusion(f32[256,8,256]{2,0,1:T(8,128)S(1)} %copy-done.5, f32[8,256,8,48]{1,3,2,0:T(8,128)S(1)} %bitcast.132, pred[]{:T(512)S(6)} %compare.5, s32[8,48]{1,0:T(8,128)S(1)} %get-tuple-element.255), kind=kOutput, calls=%fused_computation.10.clone.1 | convolution fusion | flops 2417065984 | bytes 7341569 | tf_op jit(solution)/shard_map/while/body/eval_jaxpr/scij,sjg->cig/dot_general | solution.py:122
  111.7 1.3 copy-done.6
  113.4 0.5 multiply_select_fusion.2
  113.8 0.5 copy-done
  114.7 1.3 multiply_convert_fusion.2
  116.0 1.4 convert_element_type.149
  117.4 1.8 %fusion.119 = f32[8,256,384,1]{1,2,3,0:T(8,128)S(1)} fusion(bf16[8,8,16,384]{3,2,1,0:T(8,128)(2,1)S(1)} %convert_element_type.149, bf16[32,8,16,256]{3,2,1,0:T(8,128)(2,1)} %copy-done, s32[]{:T(128)S(6)} %select_n.198), kind=kOutput, calls=%fused_computation.13.clone.1 | convolution fusion | flops 201326592 | bytes 4456452 | tf_op jit(solution)/shard_map/while/body/eval_jaxpr/stqc,stqk->sck/dot_general | solution.py:117
  119.3 3.6 %bitcast_add_fusion.2 = f32[256,8,256]{2,0,1:T(8,128)S(1)} fusion(f32[256,8,256]{2,0,1:T(8,128)S(1)} %copy-done.5, f32[8,256,8,48]{1,3,2,0:T(8,128)S(1)} %bitcast.132, pred[]{:T(512)S(6)} %compare.5, s32[8,48]{1,0:T(8,128)S(1)} %get-tuple-element.255), kind=kOutput, calls=%fused_computation.10.clone.1 | convolution fusion | flops 2417065984 | bytes 7341569 | tf_op jit(solution)/shard_map/while/body/eval_jaxpr/scij,sjg->cig/dot_general | solution.py:122
  122.9 1.3 copy-done.6
  124.5 0.5 multiply_select_fusion.2
  125.0 0.5 copy-done
  125.9 1.3 multiply_convert_fusion.2
  127.1 1.4 convert_element_type.149
  128.6 1.8 %fusion.119 = f32[8,256,384,1]{1,2,3,0:T(8,128)S(1)} fusion(bf16[8,8,16,384]{3,2,1,0:T(8,128)(2,1)S(1)} %convert_element_type.149, bf16[32,8,16,256]{3,2,1,0:T(8,128)(2,1)} %copy-done, s32[]{:T(128)S(6)} %select_n.198), kind=kOutput, calls=%fused_computation.13.clone.1 | convolution fusion | flops 201326592 | bytes 4456452 | tf_op jit(solution)/shard_map/while/body/eval_jaxpr/stqc,stqk->sck/dot_general | solution.py:117
  130.4 3.6 %bitcast_add_fusion.2 = f32[256,8,256]{2,0,1:T(8,128)S(1)} fusion(f32[256,8,256]{2,0,1:T(8,128)S(1)} %copy-done.5, f32[8,256,8,48]{1,3,2,0:T(8,128)S(1)} %bitcast.132, pred[]{:T(512)S(6)} %compare.5, s32[8,48]{1,0:T(8,128)S(1)} %get-tuple-element.255), kind=kOutput, calls=%fused_computation.10.clone.1 | convolution fusion | flops 2417065984 | bytes 7341569 | tf_op jit(solution)/shard_map/while/body/eval_jaxpr/scij,sjg->cig/dot_general | solution.py:122
  134.0 1.3 copy-done.6
  135.4 2.8 %copy.96 = f32[256,8,256]{2,1,0:T(8,128)S(1)} copy(f32[256,8,256]{2,0,1:T(8,128)} %get-tuple-element.127) | data formatting | bytes 4194304 | tf_op jit(solution)/shard_map/while | solution.py:126
  138.3 2.0 %fusion.21 = f32[1024,256]{1,0:T(8,128)S(1)} fusion(f32[1024,256]{1,0:T(8,128)S(1)} %bitcast.136), kind=kOutput, calls=%fused_computation.58 | convolution fusion | flops 806289408 | bytes 2097152 | tf_op jit(solution)/shard_map/dot_general | solution.py:39
  140.3 2.0 %fusion.20 = f32[1024,256]{1,0:T(8,128)S(1)} fusion(f32[1024,256]{1,0:T(8,128)S(1)} %bitcast.137), kind=kOutput, calls=%fused_computation.57 | convolution fusion | flops 806289408 | bytes 2097152 | tf_op jit(solution)/shard_map/dot_general | solution.py:39
  142.3 2.9 %convolution_subtract_fusion.1 = f32[1024,256]{1,0:T(8,128)} fusion(f32[1024,256]{1,0:T(8,128)S(1)} %fusion.20, f32[1024,256]{1,0:T(8,128)S(1)} %bitcast.134), kind=kOutput, calls=%fused_computation.36 | convolution fusion | flops 806551552 | bytes 3145728 | tf_op jit(solution)/shard_map/dot_general | solution.py:39
  145.2 1.4 reshape.317
  146.6 2.1 %fusion.33 = f32[64,2,2048]{2,0,1:T(8,128)} fusion(f32[2,64,2048]{2,1,0:T(8,128)S(1)} %reshape.317), kind=kOutput, calls=%fused_computation.74 | convolution fusion | flops 201388032 | bytes 2097152 | tf_op jit(solution)/shard_map/akg,kz->azg/dot_general | solution.py:43
  148.7 2.1 %fusion.37 = f32[64,2,2048]{2,0,1:T(8,128)} fusion(f32[2,64,2048]{2,1,0:T(8,128)S(1)} %reshape.317), kind=kOutput, calls=%fused_computation.78 | convolution fusion | flops 201388032 | bytes 2097152 | tf_op jit(solution)/shard_map/akg,kz->azg/dot_general | solution.py:43
  150.9 3.2 %convolution_add_fusion.1 = f32[1024,256]{1,0:T(8,128)} fusion(f32[1024,256]{1,0:T(8,128)S(1)} %fusion.21, f32[1024,256]{1,0:T(8,128)S(1)} %bitcast.135), kind=kOutput, calls=%fused_computation.35 | convolution fusion | flops 806551552 | bytes 3145728 | tf_op jit(solution)/shard_map/dot_general | solution.py:39
  154.1 1.4 reshape.318
  155.5 1.1 convolution_subtract_fusion
  156.7 1.2 convolution_add_fusion
  157.9 0.3 copy.112
  159.5 12.6 %all_to_all.35 = bf16[8,8,8,256]{3,2,1,0:T(8,128)(2,1)S(1)} all-to-all(bf16[8,8,8,256]{3,2,1,0:T(8,128)(2,1)S(1)} %copy_bitcast_fusion), channel_id=1, replica_groups=mesh['coil'=8,'spoke'=32] {'coil'}, dimensions={0} | all-to-all | bytes 524288 | tf_op jit(solution)/shard_map/all_to_all | solution.py:20
  172.1 0.7 sqrt.3
  (102 shorter events, 6.4 us)
Async XLA Ops:
  9.5 13.7 %copy-start.7 = (bf16[8,2,2,64,256]{4,3,2,1,0:T(8,128)(2,1)S(1)}, bf16[8,2,2,64,256]{4,3,2,1,0:T(8,128)(2,1)}, u32[]{:S(2)}) copy-start(bf16[8,2,2,64,256]{4,3,2,1,0:T(8,128)(2,1)} %param.11) | copy-start | bytes 3145732
  11.3 20.7 %all-to-all-start.1 = ((f32[32,1,512]{2,1,0:T(1,128)}), f32[32,1,512]{2,1,0:T(1,128)S(1)}, u32[]{:S(2)}, u32[]{:S(2)}) async-start(f32[32,1,512]{2,1,0:T(1,128)} %reshape.385), calls=%async_computation.1 | async-start | bytes 131072 | tf_op jit(solution)/shard_map/all_to_all | solution.py:91
  32.0 9.4 %copy-start.8 = (s32[32]{0:T(128)S(1)}, s32[32]{0:T(128)}, u32[]{:S(2)}) copy-start(s32[32]{0:T(128)} %param.17) | copy-start | bytes 388
  32.0 58.7 %all-to-all-start = ((bf16[8,32,16,256]{3,2,0,1:T(8,128)(2,1)}), bf16[8,32,16,256]{3,2,0,1:T(8,128)(2,1)S(1)}, u32[]{:S(2)}, u32[]{:S(2)}) async-start(bf16[8,32,16,256]{3,2,0,1:T(8,128)(2,1)} %select_bitcast_fusion), calls=%async_computation | async-start | bytes 4194304 | tf_op jit(solution)/shard_map/all_to_all | solution.py:88
  90.7 1.3 copy-start
  95.1 1.8 %copy-start.5 = (f32[256,8,256]{2,0,1:T(8,128)S(1)}, f32[256,8,256]{2,0,1:T(8,128)}, u32[]{:S(2)}) copy-start(f32[256,8,256]{2,0,1:T(8,128)} %get-tuple-element.269) | copy-start | bytes 6291460 | tf_op jit(solution)/shard_map/while
  96.9 4.9 %copy-start.1 = (bf16[32,8,16,256]{3,2,1,0:T(8,128)(2,1)S(1)}, bf16[32,8,16,256]{3,2,1,0:T(8,128)(2,1)}, u32[]{:S(2)}) copy-start(bf16[32,8,16,256]{3,2,1,0:T(8,128)(2,1)} %copy-done) | copy-start | bytes 6291460 | tf_op jit(solution)/shard_map/while
  100.5 1.3 copy-start.6
  101.9 1.3 copy-start
  106.3 1.8 %copy-start.5 = (f32[256,8,256]{2,0,1:T(8,128)S(1)}, f32[256,8,256]{2,0,1:T(8,128)}, u32[]{:S(2)}) copy-start(f32[256,8,256]{2,0,1:T(8,128)} %get-tuple-element.269) | copy-start | bytes 6291460 | tf_op jit(solution)/shard_map/while
  108.1 4.9 %copy-start.1 = (bf16[32,8,16,256]{3,2,1,0:T(8,128)(2,1)S(1)}, bf16[32,8,16,256]{3,2,1,0:T(8,128)(2,1)}, u32[]{:S(2)}) copy-start(bf16[32,8,16,256]{3,2,1,0:T(8,128)(2,1)} %copy-done) | copy-start | bytes 6291460 | tf_op jit(solution)/shard_map/while
  111.7 1.3 copy-start.6
  113.0 1.3 copy-start
  117.4 1.8 %copy-start.5 = (f32[256,8,256]{2,0,1:T(8,128)S(1)}, f32[256,8,256]{2,0,1:T(8,128)}, u32[]{:S(2)}) copy-start(f32[256,8,256]{2,0,1:T(8,128)} %get-tuple-element.269) | copy-start | bytes 6291460 | tf_op jit(solution)/shard_map/while
  119.3 4.9 %copy-start.1 = (bf16[32,8,16,256]{3,2,1,0:T(8,128)(2,1)S(1)}, bf16[32,8,16,256]{3,2,1,0:T(8,128)(2,1)}, u32[]{:S(2)}) copy-start(bf16[32,8,16,256]{3,2,1,0:T(8,128)(2,1)} %copy-done) | copy-start | bytes 6291460 | tf_op jit(solution)/shard_map/while
  122.9 1.3 copy-start.6
  124.2 1.3 copy-start
  128.6 1.8 %copy-start.5 = (f32[256,8,256]{2,0,1:T(8,128)S(1)}, f32[256,8,256]{2,0,1:T(8,128)}, u32[]{:S(2)}) copy-start(f32[256,8,256]{2,0,1:T(8,128)} %get-tuple-element.269) | copy-start | bytes 6291460 | tf_op jit(solution)/shard_map/while
  130.4 4.9 %copy-start.1 = (bf16[32,8,16,256]{3,2,1,0:T(8,128)(2,1)S(1)}, bf16[32,8,16,256]{3,2,1,0:T(8,128)(2,1)}, u32[]{:S(2)}) copy-start(bf16[32,8,16,256]{3,2,1,0:T(8,128)(2,1)} %copy-done) | copy-start | bytes 6291460 | tf_op jit(solution)/shard_map/while
  134.0 1.3 copy-start.6
  150.9 4.6 %copy-start.4 = (f32[64,2,2048]{2,0,1:T(8,128)S(1)}, f32[64,2,2048]{2,0,1:T(8,128)}, u32[]{:S(2)}) copy-start(f32[64,2,2048]{2,0,1:T(8,128)} %fusion.37) | copy-start | bytes 3145732
  155.5 1.2 copy-start.3
  159.3 13.5 %copy-start.2 = (f32[2,2,64,8,256]{4,2,1,0,3:T(8,128)}, f32[2,2,64,8,256]{4,2,1,0,3:T(8,128)S(1)}, u32[]{:S(2)}) copy-start(f32[2,2,64,8,256]{4,2,1,0,3:T(8,128)S(1)} %copy_dynamic-update-slice_fusion) | copy-start | bytes 6291460
where the time goes:
time: 174 us; the launch traced here: 173 us
  waiting for transfers between devices  46.3 us (27%)
  matrix products  38.3 us (22%)
  local copies, waits for them, and re-layouts  34.2 us (20%)
  starting transfers between devices  21.2 us (12%)
  other arithmetic  17.6 us (10%)
  blocking collectives  12.6 us (7%)
  between operations  2.31 us (1%)
    all_to_all x1, waiting for transfers between devices, on_device(): lax.all_to_all(sent_values, 'spoke', split_axis=1, concat_axis=0, tiled=T...  46.3 us
    dot_general x4, matrix products, add_block(): jnp.einsum('scij,sjg->cig', windows, placement, precision=lax.Precision.H...  14.3 us
    all_to_all x1, blocking collectives, sent_and_summed(): parts = lax.all_to_all(cut_along(shard, dim, count), axis, 0, 0, tiled=True)  12.6 us
    all_to_all x1, starting transfers between devices, on_device(): lax.all_to_all(sent_geometry, 'spoke', split_axis=1, concat_axis=0, tiled...  11.9 us
    dot_general x4, matrix products, product(): jnp.dot(left, right, precision=lax.Precision.HIGHEST, preferred_element_t...  10.1 us
    all_to_all x1, starting transfers between devices, on_device(): lax.all_to_all(sent_values, 'spoke', split_axis=1, concat_axis=0, tiled=T...  9.35 us
    while x32, local copies, waits for them, and re-layouts  7.46 us
    dot_general x4, matrix products, add_block(): jnp.einsum('stqc,stqk->sck', values, weights, preferred_element_type=jnp....  7.24 us
  transfers between devices with their start and end apart: 2, of which 1 were waited for; matrix products, arithmetic and copies ran while one was open for 6% of the time, Pallas kernels for 0%

commit v1 on v0

v1 whole, which is shorter than its diff:
```python
import math

import jax
import jax.numpy as jnp
import numpy as np
from jax import lax
from jax.experimental import pallas as pl
from jax.experimental.pallas import tpu as pltpu
from jax.sharding import PartitionSpec as P

MESH = pl.DeviceIdType.MESH
FW = 32
REACH = 2
COIL_DEV = 8
SPOKE_DEV = 32
X_DEV = 4
Z_DEV = 8
SLOTS = 8
ROWS = 8
BLOCK = ROWS + 2 * REACH
PAIRS = BLOCK // 2
COLS = 128
GROUPS = 4
PER = SPOKE_DEV // GROUPS
BAND = 3 * 16 * PER
F32 = jnp.float32
BF16 = jnp.bfloat16


def kernel(distance):
    inner = jnp.maximum(1.0 - distance * distance * 0.25, 0.0)
    return inner * inner


def depth_table(length):
    phase = 2.0 * np.pi / length * (np.outer(np.arange(length), np.arange(length)) % length)
    c, s = np.cos(phase) / math.sqrt(length), np.sin(phase) / math.sqrt(length)
    return np.block([[c, -s], [s, c]])


def column_table(length):
    phase = 2.0 * np.pi / length * (np.outer(np.arange(length), np.arange(length)) % length)
    return np.concatenate([np.cos(phase), np.sin(phase)], axis=1) / math.sqrt(length)


def thirds(x):
    high = x.astype(BF16)
    rest = x - high.astype(F32)
    mid = rest.astype(BF16)
    low = (rest - mid.astype(F32)).astype(BF16)
    return high, mid, low


def dot_nt(a, b):
    return lax.dot_general(a, b, (((1,), (1,)), ((), ())), preferred_element_type=F32)


def dot(a, b):
    return jnp.dot(a, b, preferred_element_type=F32)


def body(
    owner_ref, live_ref, kdata_hbm, select_ref, place_ref, coords_ref, foot_ref, table_ref, index_ref, depth_ref, column_ref,
    images_hbm, combined_ref,
    kd, stage, send, recv, geo_send, geo, weights, fold, grid, images, power, power_send, power_recv,
    kd_sem, geo_ssem, geo_rsem, pass_ssem, pass_rsem, val_ssem, val_rsem, pow_ssem, pow_rsem, out_sem,
):
    me = lax.axis_index("spoke")
    coil = lax.axis_index("coil")
    x, z = me // Z_DEV, lax.rem(me, Z_DEV)

    def away(slot, sign):
        r = lax.rem(slot, Z_DEV)
        odd = lax.rem(r, 2)
        dz = lax.rem(odd * ((r + 1) // 2) + (1 - odd) * (Z_DEV - r // 2), Z_DEV)
        dx = slot // Z_DEV
        return lax.rem(x + sign * dx + X_DEV, X_DEV) * Z_DEV + lax.rem(z + sign * dz + Z_DEV, Z_DEV)

    load = pltpu.make_async_copy(kdata_hbm, kd, kd_sem)
    load.start()

    barrier = pltpu.get_barrier_semaphore()

    @pl.loop(1, SPOKE_DEV)
    def _(slot):
        pl.semaphore_signal(barrier, inc=1, device_id=(coil, away(slot, 1)), device_id_type=MESH)

    @pl.loop(1, COIL_DEV)
    def _(step):
        pl.semaphore_signal(barrier, inc=1, device_id=(lax.rem(coil + step, COIL_DEV), me), device_id_type=MESH)

    row_of = lax.broadcasted_iota(jnp.int32, (8, 256), 0)
    lane_of = lax.broadcasted_iota(jnp.int32, (8, 256), 1)
    high, mid, low = thirds(jnp.broadcast_to(table_ref[...], (8, 256)))
    table3 = jnp.where(
        row_of == 0,
        high.astype(F32),
        jnp.where(row_of == 1, mid.astype(F32), jnp.where(row_of == 2, low.astype(F32), 0.0)),
    ).astype(BF16)
    entry = lax.broadcasted_iota(jnp.int32, (256, 256), 0)
    density = jnp.zeros((8, 256), F32)
    for p in range(SLOTS):
        hit = jnp.where(entry == index_ref[p : p + 1, :], 1.0, 0.0).astype(BF16)
        looked = jnp.sum(dot(table3, hit), axis=0, keepdims=True)
        density = density + jnp.where(row_of == p, looked, 0.0)
    density = jnp.where(row_of < live_ref[0], density, 0.0)
    parts = []
    for comp in (coords_ref[0], coords_ref[1], density, foot_ref[...]):
        parts.extend(t.astype(F32) for t in thirds(comp))
    geometry = jnp.concatenate(parts, axis=0).astype(BF16)
    sample = lax.broadcasted_iota(jnp.int32, (256, 128), 0)
    group_of = lax.broadcasted_iota(jnp.int32, (8, 128), 1) // 32
    for t in range(GROUPS):
        dest = away(t * 8 + coil, 1)
        hit = jnp.where(sample == place_ref[pl.ds(dest, 1), :], 1.0, 0.0).astype(BF16)
        got = dot(geometry, hit)
        tile = jnp.zeros((8, 128), F32)
        for c in range(4):
            part = got[24 * c : 24 * c + 8] + got[24 * c + 8 : 24 * c + 16] + got[24 * c + 16 : 24 * c + 24]
            tile = jnp.where(group_of == c, part, tile)
        geo_send[t] = tile

    def fill(c):
        for p in range(SLOTS):
            stage[pl.ds(p, SPOKE_DEV * BLOCK, stride=SLOTS), :] = dot_nt(
                select_ref[...], kd[p, c * COLS : (c + 1) * COLS, :]
            )
        send[c] = stage[...].astype(BF16).reshape(SPOKE_DEV, BLOCK * SLOTS, COLS)

    load.wait()
    fill(0)

    pl.semaphore_wait(barrier, SPOKE_DEV - 1 + COIL_DEV - 1)

    def geo_copy(t):
        return pltpu.make_async_remote_copy(
            geo_send.at[t],
            geo.at[coil, t],
            geo_ssem.at[t],
            geo_rsem.at[t],
            device_id=(coil, away(t * 8 + coil, 1)),
            device_id_type=MESH,
        )

    def value_copy(c, slot):
        dest = away(slot, 1)
        return pltpu.make_async_remote_copy(
            send.at[c, dest],
            recv.at[c, slot],
            val_ssem.at[c, slot],
            val_rsem.at[c, slot],
            device_id=(coil, dest),
            device_id_type=MESH,
        )

    def pass_copy(step):
        return pltpu.make_async_remote_copy(
            geo.at[coil],
            geo.at[coil],
            pass_ssem.at[step],
            pass_rsem.at[step],
            device_id=(lax.rem(coil + step, COIL_DEV), me),
            device_id_type=MESH,
        )

    def pass_arrival(step):
        source = lax.rem(coil - step + COIL_DEV, COIL_DEV)
        return pltpu.make_async_remote_copy(
            geo.at[source],
            geo.at[source],
            pass_ssem.at[step],
            pass_rsem.at[step],
            device_id=(lax.rem(coil + step, COIL_DEV), me),
            device_id_type=MESH,
        )

    for t in range(1, GROUPS):
        geo_copy(t).start()

    @pl.when(coil != 0)
    def _():
        geo_copy(0).start()

    @pl.when(coil == 0)
    def _():
        geo[0, 0] = geo_send[0]

    @pl.loop(1, SPOKE_DEV)
    def _(slot):
        value_copy(0, slot).start()

    fill(1)

    @pl.loop(1, SPOKE_DEV)
    def _(slot):
        value_copy(1, slot).start()

    recv[0, 0] = send[0, me]
    recv[1, 0] = send[1, me]

    for t in range(1, GROUPS):
        geo_copy(t).wait_recv()

    @pl.when(coil != 0)
    def _():
        geo_copy(0).wait_recv()

    @pl.loop(1, COIL_DEV)
    def _(step):
        pass_copy(step).start()

    @pl.loop(1, COIL_DEV)
    def _(step):
        pass_arrival(step).wait_recv()

    first_row = (owner_ref[me] * ROWS).astype(F32)
    cells = lax.broadcasted_iota(jnp.int32, (8, 256), 1).astype(F32)

    @pl.loop(0, SPOKE_DEV)
    def _(slot):
        group = slot // PER
        member = lax.rem(slot, PER)
        tile = geo[lax.rem(slot, 8), slot // 8]

        def spread(comp, j):
            lane = comp * 32 + j
            return jnp.broadcast_to(tile[:, lane : lane + 1], (8, 256))

        across, along = [], []
        for j in range(BLOCK):
            start = spread(3, j)
            covered = (cells >= start) & (cells < start + FW)
            across.append(jnp.where(covered, kernel(cells + 0.5 - spread(1, j)), 0.0))
            along.append((spread(0, j)[:, :128], spread(2, j)[:, :128]))
        at = pl.multiple_of(member * 16, 16)
        for g in range(ROWS):
            for i in range(3):
                pair = []
                for j in (2 * (g // 2 + i), 2 * (g // 2 + i) + 1):
                    row, dens = along[j]
                    value = dens * kernel(first_row + (g + 0.5) - row)
                    pair.append(jnp.concatenate([value, value], axis=1) * across[j])
                weights[group, g, pl.ds(i * 16 * PER + at, 16), :] = jnp.concatenate(pair, axis=0).astype(BF16)

    for c in range(2):
        for q in range(GROUPS):

            @pl.loop(max(1, q * PER), (q + 1) * PER)
            def _(slot):
                value_copy(c, slot).wait_recv()

            for i in range(PAIRS):
                got = recv[c, q * PER : (q + 1) * PER, i * 16 : (i + 1) * 16, :].reshape(16 * PER, COLS)
                folded = dot_nt(depth_ref[0], got) + dot_nt(depth_ref[1], got)
                fold[:, i * 16 * PER : (i + 1) * 16 * PER] = folded.astype(BF16)
            for g in range(ROWS):
                at = (g // 2) * 16 * PER
                term = dot(fold[:, at : at + BAND], weights[q, g])
                grid[g] = term if q == 0 else grid[g] + term
        for h in range(ROWS // 2):
            pair = []
            for g in (2 * h, 2 * h + 1):
                turned = dot(grid[g].astype(BF16), column_ref[...])
                real = turned[:64, :256] - turned[64:, 256:]
                imag = turned[:64, 256:] + turned[64:, :256]
                images[g, c, 0] = real
                images[g, c, 1] = imag
                mine = real * real + imag * imag
                if c == 0:
                    power[g] = mine
                else:
                    pair.append(power[g] + mine)
            out = pltpu.make_async_copy(
                images.at[pl.ds(2 * h, 2), c], images_hbm.at[pl.ds(2 * h, 2), c], out_sem.at[c, h]
            )
            out.start()
            if c == 1:
                for k in range(COIL_DEV):
                    power_send[h, k] = jnp.concatenate([m[8 * k : 8 * k + 8] for m in pair], axis=0).astype(BF16)

                @pl.loop(1, COIL_DEV)
                def _(step):
                    power_copy(power_send, power_recv, pow_ssem, pow_rsem, coil, me, h, step).start()

    for h in range(ROWS // 2):
        power_recv[h, 0] = power_send[h, coil]

        @pl.loop(1, COIL_DEV)
        def _(step):
            power_copy(power_send, power_recv, pow_ssem, pow_rsem, coil, me, h, step).wait_recv()

        total = power_recv[h, 0].astype(F32)
        for k in range(1, COIL_DEV):
            total = total + power_recv[h, k].astype(F32)
        combined = jnp.sqrt(total)
        combined_ref[2 * h] = combined[:8]
        combined_ref[2 * h + 1] = combined[8:]

    for c in range(2):
        for h in range(ROWS // 2):
            pltpu.make_async_copy(
                images.at[pl.ds(2 * h, 2), c], images_hbm.at[pl.ds(2 * h, 2), c], out_sem.at[c, h]
            ).wait()

        @pl.loop(1, SPOKE_DEV)
        def _(slot):
            value_copy(c, slot).wait_send()

    for t in range(1, GROUPS):
        geo_copy(t).wait_send()

    @pl.when(coil != 0)
    def _():
        geo_copy(0).wait_send()

    @pl.loop(1, COIL_DEV)
    def _(step):
        pass_copy(step).wait_send()
        for h in range(ROWS // 2):
            power_copy(power_send, power_recv, pow_ssem, pow_rsem, coil, me, h, step).wait_send()


def power_copy(power_send, power_recv, ssem, rsem, coil, me, h, step):
    peer = lax.rem(coil + step, COIL_DEV)
    return pltpu.make_async_remote_copy(
        power_send.at[h, peer],
        power_recv.at[h, step],
        ssem.at[h, step],
        rsem.at[h, step],
        device_id=(peer, me),
        device_id_type=MESH,
    )


def on_device(kdata, coords, foot_offset, live_count, dcf_table, dcf_index, slab_owner):
    slots, coil_dev, parts, kz, samp = kdata.shape
    kd = kdata.reshape(slots, coil_dev * parts * kz, samp)
    first = slab_owner * ROWS - REACH
    wanted = (first[:, None] + jnp.arange(BLOCK, dtype=jnp.int32)[None, :]).reshape(-1)
    select = (wanted[:, None] == jnp.arange(samp, dtype=jnp.int32)[None, :]).astype(BF16)
    lane = jnp.arange(128, dtype=jnp.int32)[None, :]
    place = jnp.where(
        lane >= 96,
        slab_owner[:, None],
        jnp.where(lane % 32 < BLOCK, first[:, None] + lane % 32, -1),
    )
    table = jnp.pad(dcf_table, (0, 256 - dcf_table.shape[0])).reshape(1, 256)
    foot = jnp.pad(foot_offset.astype(F32), ((0, 0), (0, 256 - foot_offset.shape[1])))
    exact = depth_table(kz)
    coarse = np.asarray(exact, BF16)
    depth = jnp.asarray(np.stack([coarse, np.asarray(exact - coarse.astype(np.float64), BF16)]))
    column = jnp.asarray(column_table(samp), BF16)
    vmem = pl.BlockSpec(memory_space=pltpu.VMEM)
    smem = pl.BlockSpec(memory_space=pltpu.SMEM)
    hbm = pl.BlockSpec(memory_space=pl.ANY)
    dma = pltpu.SemaphoreType.DMA
    images, combined = pl.pallas_call(
        body,
        out_shape=(
            jax.ShapeDtypeStruct((ROWS, coil_dev, parts, kz, samp), F32),
            jax.ShapeDtypeStruct((ROWS, kz // COIL_DEV, samp), F32),
        ),
        in_specs=[smem, smem, hbm] + [vmem] * 8,
        out_specs=(hbm, vmem),
        scratch_shapes=[
            pltpu.VMEM((slots, coil_dev * parts * kz, samp), BF16),
            pltpu.VMEM((SPOKE_DEV * BLOCK * SLOTS, COLS), F32),
            pltpu.VMEM((2, SPOKE_DEV, BLOCK * SLOTS, COLS), BF16),
            pltpu.VMEM((2, SPOKE_DEV, BLOCK * SLOTS, COLS), BF16),
            pltpu.VMEM((GROUPS, 8, 128), F32),
            pltpu.VMEM((COIL_DEV, GROUPS, 8, 128), F32),
            pltpu.VMEM((GROUPS, ROWS, BAND, 256), BF16),
            pltpu.VMEM((COLS, PAIRS * 16 * PER), BF16),
            pltpu.VMEM((ROWS, COLS, 256), F32),
            pltpu.VMEM((ROWS, coil_dev, parts, kz, samp), F32),
            pltpu.VMEM((ROWS, kz, samp), F32),
            pltpu.VMEM((ROWS // 2, COIL_DEV, 16, samp), BF16),
            pltpu.VMEM((ROWS // 2, COIL_DEV, 16, samp), BF16),
            dma,
            dma((GROUPS,)),
            dma((GROUPS,)),
            dma((COIL_DEV,)),
            dma((COIL_DEV,)),
            dma((2, SPOKE_DEV)),
            dma((2, SPOKE_DEV)),
            dma((ROWS // 2, COIL_DEV)),
            dma((ROWS // 2, COIL_DEV)),
            dma((2, ROWS // 2)),
        ],
        compiler_params=pltpu.CompilerParams(
            collective_id=0, has_side_effects=True, vmem_limit_bytes=56 * 2**20
        ),
    )(
        slab_owner,
        live_count,
        kd,
        select,
        place,
        jnp.transpose(coords, (1, 0, 2)),
        foot,
        table,
        dcf_index,
        depth,
        column,
    )
    return images, combined


def solution(mesh):
    return jax.shard_map(
        on_device,
        mesh=mesh,
        in_specs=(
            P("spoke", "coil", None, None, None),
            P("spoke", None, None),
            P("spoke", None),
            P("spoke"),
            P(),
            P("spoke", None),
            P(),
        ),
        out_specs=(P("spoke", "coil", None, None, None), P("spoke", "coil", None)),
        check_vma=False,
    )
```

time: 174 us -> 70.5 us (0.41)
  Pallas kernels: 0 us -> 58.3 us
  waiting for transfers between devices: 46.3 us -> 0 us
  matrix products: 38.3 us -> 0 us
  local copies, waits for them, and re-layouts: 34.2 us -> 7.07 us
  starting transfers between devices: 21.2 us -> 0 us
  other arithmetic: 17.6 us -> 3.56 us
  blocking collectives: 12.6 us -> 0 us
    pallas_call x0 -> x1, Pallas kernels: none -> 58.3 us  [on_device(): pl.pallas_call(body, out_shape=(jax.ShapeDtypeStruct((ROWS, coil_dev, par...]
    all_to_all x2 -> x0, waiting for transfers between devices: 46.3 us -> none  [the longest x1 46.3 us: on_device(): lax.all_to_all(sent_values, 'spoke', split_axis=1, concat_axis=0, tiled=T...]
    dot_general x16 -> x0, matrix products: 38.3 us -> none  [the longest x4 14.3 us: add_block(): jnp.einsum('scij,sjg->cig', windows, placement, precision=lax.Precision.H...]
    all_to_all x2 -> x0, starting transfers between devices: 21.2 us -> none  [the longest x1 11.9 us: on_device(): lax.all_to_all(sent_geometry, 'spoke', split_axis=1, concat_axis=0, tiled...]
    all_to_all x1 -> x0, blocking collectives: 12.6 us -> none  [sent_and_summed(): parts = lax.all_to_all(cut_along(shard, dim, count), axis, 0, 0, tiled=True)]
    while x33 -> x0, local copies, waits for them, and re-layouts: 10.3 us -> none
    gather x7 -> x0, local copies, waits for them, and re-layouts: 7.87 us -> none  [the longest x2 2.16 us: on_device(): jnp.take(samples_last, clipped, axis=1)]
    convert_element_type x5 -> x0, local copies, waits for them, and re-layouts: 5.87 us -> none  [the longest x4 5.79 us: add_block(): weights = (row_weight[..., None] * col_weight[..., None, :]).reshape(send...]
  transfers between devices with their start and end apart: 2 -> 0, of which waited for: 1 -> 0; matrix products, arithmetic and copies ran while one was open for 6% -> 0% of each run, Pallas kernels for 0% -> 0%
where the time goes in v1:
time: 70.5 us; the launch traced here: 70.2 us
  Pallas kernels  58.3 us (83%)
  local copies, waits for them, and re-layouts  7.07 us (10%)
  other arithmetic  3.56 us (5%)
  between operations  1.3 us (2%)
    pallas_call x1, Pallas kernels, on_device(): pl.pallas_call(body, out_shape=(jax.ShapeDtypeStruct((ROWS, coil_dev, par...  58.3 us
    unnamed x5, local copies, waits for them, and re-layouts  5.11 us

profile of v1, /device:TPU:1, one launch (start us, length us, event | category | flops | bytes accessed | tf_op | source)
XLA Modules:
  0.0 70.2 jit_solution(11317630125306848829)
XLA Ops:
  1.3 0.7 multiply_add_fusion
  1.9 1.3 %pad.9 = f32[256]{0:T(256)} pad(f32[129]{0:T(256)} %param.13, f32[]{:T(128)} %constant.36.clone.1), padding=0_127 | pad | bytes 1544 | tf_op jit(solution)/shard_map/jit(_pad)/pad | solution.py:347
  3.2 0.7 convert_element_type.11
  3.9 0.6 pad.8.foot_ref
  4.5 1.3 %select_select_fusion.place_ref = s32[32,128]{1,0:T(8,128)} fusion(s32[128]{0:T(128)S(1)} %and_select_fusion, s32[32]{0:T(128)S(1)} %multiply_add_fusion, s32[32]{0:T(128)} %owner_ref.1, pred[128]{0:T(512)(128)(4,1)S(1)} %get-tuple-element.3, pred[128]{0:T(512)(128)(4,1)S(1)} %get-tuple-element.2), kind=kLoop, calls=%fused_computation.3 | loop fusion | flops 12288 | bytes 17408 | tf_op jit(solution)/shard_map/jit(_where)/select_n | solution.py:342
  5.8 0.1 iota_add_fusion
  5.9 0.1 add.59
  6.0 1.3 %copy.14 = f32[8,2,256]{2,0,1:T(8,128)} copy(f32[8,2,256]{2,1,0:T(2,128)} %param.10) | data formatting | bytes 32768 | tf_op args[1]
  7.3 0.8 %fusion.select_ref = bf16[384,256]{1,0:T(8,128)(2,1)} fusion(s32[384]{0:T(512)S(1)} %add.59), kind=kLoop, calls=%fused_computation.1 | loop fusion | flops 196608 | bytes 198144 | tf_op jit(solution)/shard_map/convert_element_type | solution.py:340
  8.1 58.3 %shard_map.104 = (f32[8,2,2,64,256]{4,3,2,1,0:T(8,128)}, f32[8,8,256]{2,1,0:T(8,128)}) custom-call(s32[32]{0:T(128)} %owner_ref.1, s32[1]{0:T(128)S(6)} %copy.17.live_ref, bf16[8,256,256]{2,1,0:T(8,128)(2,1)} %bitcast.5, bf16[384,256]{1,0:T(8,128)(2,1)} %fusion.select_ref, s32[32,128]{1,0:T(8,128)} %select_select_fusion.place_ref, f32[2,8,256]{2,1,0:T(8,128)} %bitcast.6, ...), custom_call_target="tpu_custom_call" | custom-call | tf_op jit(solution)/shard_map/pallas_call | solution.py:357
  66.4 0.0 copy-start
  66.4 3.2 %copy.18 = f32[8,2,2,64,256]{4,3,2,1,0:T(8,128)} copy(f32[8,2,2,64,256]{4,3,2,1,0:T(8,128)} %get-tuple-element.6) | data formatting | bytes 4194304
  69.6 0.0 copy-done
  69.6 0.6 copy.19
  (2 shorter events, 0.0 us)
Async XLA Ops:
  66.4 3.2 %copy-start = (f32[8,8,256]{2,1,0:T(8,128)S(1)}, f32[8,8,256]{2,1,0:T(8,128)}, u32[]{:S(2)}) copy-start(f32[8,8,256]{2,1,0:T(8,128)} %get-tuple-element.7) | copy-start | bytes 196612

commit v2 on v1

v2 whole, which is shorter than its diff:
```python
import math

import jax
import jax.numpy as jnp
import numpy as np
from jax import lax
from jax.experimental import pallas as pl
from jax.experimental.pallas import tpu as pltpu
from jax.sharding import PartitionSpec as P

MESH = pl.DeviceIdType.MESH
FW = 32
REACH = 2
COIL_DEV = 8
SPOKE_DEV = 32
X_DEV = 4
Z_DEV = 8
SLOTS = 8
Z_ORDER = (0, 1, 7, 2, 6, 3, 5, 4)
ROWS = 8
BLOCK = ROWS + 2 * REACH
PAIRS = BLOCK // 2
EARLY = SLOTS * (BLOCK - 2)
COLS = 128
GROUPS = 4
PER = SPOKE_DEV // GROUPS
BAND = 3 * 16 * PER
F32 = jnp.float32
BF16 = jnp.bfloat16


def kernel(distance):
    inner = jnp.maximum(1.0 - distance * distance * 0.25, 0.0)
    return inner * inner


def depth_table(length):
    phase = 2.0 * np.pi / length * (np.outer(np.arange(length), np.arange(length)) % length)
    c, s = np.cos(phase) / math.sqrt(length), np.sin(phase) / math.sqrt(length)
    return np.block([[c, -s], [s, c]])


def column_table(length):
    phase = 2.0 * np.pi / length * (np.outer(np.arange(length), np.arange(length)) % length)
    c, s = np.cos(phase) / math.sqrt(length), np.sin(phase) / math.sqrt(length)
    return np.block([[c, s], [-s, c]])


def in_two(exact):
    coarse = np.asarray(exact, BF16)
    return jnp.asarray(np.stack([coarse, np.asarray(exact - coarse.astype(np.float64), BF16)]))


def thirds(x):
    high = x.astype(BF16)
    rest = x - high.astype(F32)
    mid = rest.astype(BF16)
    low = (rest - mid.astype(F32)).astype(BF16)
    return high, mid, low


def dot_nt(a, b):
    return lax.dot_general(a, b, (((1,), (1,)), ((), ())), preferred_element_type=F32)


def dot(a, b):
    return jnp.dot(a, b, preferred_element_type=F32)


def body(
    live_ref, owner_hbm, table_hbm, coords_hbm, foot_hbm, index_hbm, kdata_hbm, depth_hbm, column_hbm,
    images, combined_ref,
    owner_ref, table_ref, coords_ref, foot_ref, index_ref, kd, depth_ref, column_ref, select, stage, send, recv, geo_send, geo, weights, fold, grid, power, power_send, power_recv,
    load_sem, geo_ssem, geo_rsem, pass_ssem, pass_rsem, val_ssem, val_rsem, pow_ssem, pow_rsem,
):
    me = lax.axis_index("spoke")
    coil = lax.axis_index("coil")
    x, z = me // Z_DEV, lax.rem(me, Z_DEV)
    x_at = [lax.rem(x + dx, X_DEV) * Z_DEV for dx in range(X_DEV)]
    z_at = [lax.rem(z + dz, Z_DEV) for dz in range(Z_DEV)]
    coil_at = [lax.rem(coil + step, COIL_DEV) for step in range(COIL_DEV)]

    def away(slot):
        return x_at[slot // Z_DEV] + z_at[Z_ORDER[slot % Z_DEV]]

    barrier = pltpu.get_barrier_semaphore()
    for slot in reversed(range(1, SPOKE_DEV)):
        pl.semaphore_signal(barrier, inc=1, device_id=(coil, away(slot)), device_id_type=MESH)
    for step in range(1, COIL_DEV):
        pl.semaphore_signal(barrier, inc=1, device_id=(coil_at[step], me), device_id_type=MESH)

    held = (owner_ref, table_ref, coords_ref, foot_ref, index_ref, kd, depth_ref, column_ref)
    given = (owner_hbm, table_hbm, coords_hbm, foot_hbm, index_hbm, kdata_hbm, depth_hbm, column_hbm)
    loads = [pltpu.make_async_copy(a, b, load_sem.at[i]) for i, (a, b) in enumerate(zip(given, held))]
    for load in loads:
        load.start()

    for load in loads[:5]:
        load.wait()
    row_of = lax.broadcasted_iota(jnp.int32, (8, 256), 0)
    entry = index_ref[...]
    density = jnp.zeros((8, 256), F32)
    for n in range(table_ref.shape[0]):
        density = jnp.where(entry == n, table_ref[n], density)
    density = jnp.where(row_of < live_ref[0], density, 0.0)
    foot = jnp.concatenate([foot_ref[...].astype(F32), jnp.zeros((8, 256 - SPOKE_DEV), F32)], axis=1)
    parts = []
    for comp in (coords_ref[:, 0, :], coords_ref[:, 1, :], density, foot):
        parts.extend(t.astype(F32) for t in thirds(comp))
    geometry = jnp.concatenate(parts, axis=0).astype(BF16)
    sample = lax.broadcasted_iota(jnp.int32, (256, 128), 0)
    lane = lax.broadcasted_iota(jnp.int32, (256, 128), 1)
    offset = lax.rem(lane, 32)
    group_of = lax.broadcasted_iota(jnp.int32, (8, 128), 1) // 32
    half, odd = (coil + 1) // 2, lax.rem(coil, 2)
    z_geo = lax.rem(z + odd * half + (1 - odd) * (Z_DEV - half), Z_DEV)
    for t in range(GROUPS):
        slab = owner_ref[x_at[t] + z_geo]
        near = (lane < 96) & (offset < BLOCK) & (sample == slab * ROWS - REACH + offset)
        hit = jnp.where(near | ((lane >= 96) & (sample == slab)), 1.0, 0.0).astype(BF16)
        got = dot(geometry, hit)
        tile = jnp.zeros((8, 128), F32)
        for c in range(4):
            part = got[24 * c : 24 * c + 8] + got[24 * c + 8 : 24 * c + 16] + got[24 * c + 16 : 24 * c + 24]
            tile = jnp.where(group_of == c, part, tile)
        geo_send[t] = tile

    row = lax.broadcasted_iota(jnp.int32, (4 * BLOCK, 256), 0)
    column = lax.broadcasted_iota(jnp.int32, (4 * BLOCK, 256), 1)
    for b in range(SPOKE_DEV // 4):
        wanted = owner_ref[4 * b] * ROWS - REACH + row
        for k in range(1, 4):
            wanted = jnp.where(row >= k * BLOCK, owner_ref[4 * b + k] * ROWS - REACH - k * BLOCK + row, wanted)
        select[b * 4 * BLOCK : (b + 1) * 4 * BLOCK, :] = jnp.where(wanted == column, 1.0, 0.0).astype(BF16)

    def fill(c):
        for p in range(SLOTS):
            stage[pl.ds(p, SPOKE_DEV * BLOCK, stride=SLOTS), :] = dot_nt(
                select[...], kd[p, c * COLS : (c + 1) * COLS, :]
            )
        send[:, :, c * COLS : (c + 1) * COLS] = stage[...].astype(BF16).reshape(SPOKE_DEV, BLOCK * SLOTS, COLS)

    loads[5].wait()
    fill(0)
    fill(1)

    pl.semaphore_wait(barrier, SPOKE_DEV - 1 + COIL_DEV - 1)

    def geo_copy(t):
        return pltpu.make_async_remote_copy(
            geo_send.at[t],
            geo.at[coil, t],
            geo_ssem.at[t],
            geo_rsem.at[t],
            device_id=(coil, x_at[t] + z_geo),
            device_id_type=MESH,
        )

    def value_copy(c, slot, dest):
        rows = (pl.ds(0, EARLY), pl.ds(EARLY, BLOCK * SLOTS - EARLY))[c]
        return pltpu.make_async_remote_copy(
            send.at[dest, rows],
            recv.at[slot, rows],
            val_ssem.at[c, slot],
            val_rsem.at[c, slot],
            device_id=(coil, dest),
            device_id_type=MESH,
        )

    def pass_copy(step):
        return pltpu.make_async_remote_copy(
            geo.at[coil],
            geo.at[coil],
            pass_ssem.at[step],
            pass_rsem.at[step],
            device_id=(lax.rem(coil + step, COIL_DEV), me),
            device_id_type=MESH,
        )

    def pass_arrival(step):
        source = lax.rem(coil - step + COIL_DEV, COIL_DEV)
        return pltpu.make_async_remote_copy(
            geo.at[source],
            geo.at[source],
            pass_ssem.at[step],
            pass_rsem.at[step],
            device_id=(lax.rem(coil + step, COIL_DEV), me),
            device_id_type=MESH,
        )

    for t in range(1, GROUPS):
        geo_copy(t).start()

    @pl.when(coil != 0)
    def _():
        geo_copy(0).start()

    @pl.when(coil == 0)
    def _():
        geo[0, 0] = geo_send[0]

    for c in range(2):
        for slot in range(1, SPOKE_DEV):
            value_copy(c, slot, away(slot)).start()

    recv[0] = send[me]

    for t in range(1, GROUPS):
        geo_copy(t).wait_recv()

    @pl.when(coil != 0)
    def _():
        geo_copy(0).wait_recv()

    @pl.loop(1, COIL_DEV)
    def _(step):
        pass_copy(step).start()

    @pl.loop(1, COIL_DEV)
    def _(step):
        pass_arrival(step).wait_recv()

    first_row = (owner_ref[me] * ROWS).astype(F32)
    cells = lax.broadcasted_iota(jnp.int32, (8, 256), 1).astype(F32)

    @pl.loop(0, SPOKE_DEV)
    def _(slot):
        group = slot // PER
        member = lax.rem(slot, PER)
        tile = geo[lax.rem(slot, 8), slot // 8]

        def spread(comp, j):
            lane = comp * 32 + j
            return jnp.broadcast_to(tile[:, lane : lane + 1], (8, 256))

        across, along = [], []
        for j in range(BLOCK):
            start = spread(3, j)
            covered = (cells >= start) & (cells < start + FW)
            across.append(jnp.where(covered, kernel(cells + 0.5 - spread(1, j)), 0.0))
            along.append((spread(0, j)[:, :128], spread(2, j)[:, :128]))
        at = pl.multiple_of(member * 16, 16)
        for g in range(ROWS):
            for i in range(3):
                pair = []
                for j in (2 * (g // 2 + i), 2 * (g // 2 + i) + 1):
                    row, dens = along[j]
                    value = dens * kernel(first_row + (g + 0.5) - row)
                    pair.append(jnp.concatenate([value, value], axis=1) * across[j])
                weights[group, g, pl.ds(i * 16 * PER + at, 16), :] = jnp.concatenate(pair, axis=0).astype(BF16)

    for load in loads[6:]:
        load.wait()

    def arrived(c, q):
        @pl.loop(max(1, q * PER), (q + 1) * PER)
        def _(slot):
            value_copy(c, slot, x_at[1]).wait_recv()

    def folded(i, q, c):
        got = recv[q * PER : (q + 1) * PER, i * 16 : (i + 1) * 16, c * COLS : (c + 1) * COLS].reshape(16 * PER, COLS)
        both = dot_nt(depth_ref[0], got) + dot_nt(depth_ref[1], got)
        fold[:, i * 16 * PER : (i + 1) * 16 * PER] = both.astype(BF16)

    def transform(c, h):
        spectrum = jnp.concatenate(
            [jnp.concatenate([grid[c, g, :64], grid[c, g, 64:]], axis=1) for g in (2 * h, 2 * h + 1)], axis=0
        ).astype(BF16)
        turned = dot(spectrum, column_ref[0]) + dot(spectrum, column_ref[1])
        for g in (2 * h, 2 * h + 1):
            at = (g - 2 * h) * 64
            real, imag = turned[at : at + 64, :256], turned[at : at + 64, 256:]
            images[g, c, 0] = real
            images[g, c, 1] = imag
            mine = real * real + imag * imag
            power[g] = mine if c == 0 else power[g] + mine

    def share(h):
        for k in range(COIL_DEV):
            power_send[h, k] = jnp.concatenate(
                [power[g, 8 * k : 8 * k + 8] for g in (2 * h, 2 * h + 1)], axis=0
            ).astype(BF16)
        for step in range(1, COIL_DEV):
            power_copy(h, step).start()

    def power_copy(h, step):
        return pltpu.make_async_remote_copy(
            power_send.at[h, coil_at[step]],
            power_recv.at[h, step],
            pow_ssem.at[h, step],
            pow_rsem.at[h, step],
            device_id=(coil_at[step], me),
            device_id_type=MESH,
        )

    last = PAIRS - 1
    for q in range(GROUPS):
        arrived(0, q)
        for c in range(2):
            for i in range(last):
                folded(i, q, c)
            for g in range(ROWS):
                depth = BAND if g // 2 + 2 < last else BAND - 16 * PER
                at = (g // 2) * 16 * PER
                term = dot(fold[:, at : at + depth], weights[q, g, :depth])
                grid[c, g] = term if q == 0 else grid[c, g] + term
    for h in range(ROWS // 2 - 1):
        transform(0, h)
        transform(1, h)
        share(h)
    for q in range(GROUPS):
        arrived(1, q)
        for c in range(2):
            folded(last, q, c)
            got = fold[:, last * 16 * PER :]
            for g in (ROWS - 2, ROWS - 1):
                grid[c, g] = grid[c, g] + dot(got, weights[q, g, BAND - 16 * PER :])
    for c in range(2):
        transform(c, ROWS // 2 - 1)
    share(ROWS // 2 - 1)

    for h in range(ROWS // 2):
        power_recv[h, 0] = power_send[h, coil]
        for step in range(1, COIL_DEV):
            power_copy(h, step).wait_recv()
        total = power_recv[h, 0].astype(F32)
        for k in range(1, COIL_DEV):
            total = total + power_recv[h, k].astype(F32)
        combined = jnp.sqrt(total)
        combined_ref[2 * h] = combined[:8]
        combined_ref[2 * h + 1] = combined[8:]

    for c in range(2):

        @pl.loop(1, SPOKE_DEV)
        def _(slot):
            value_copy(c, slot, x_at[1]).wait_send()

    for t in range(1, GROUPS):
        geo_copy(t).wait_send()

    @pl.when(coil != 0)
    def _():
        geo_copy(0).wait_send()

    @pl.loop(1, COIL_DEV)
    def _(step):
        pass_copy(step).wait_send()

    for h in range(ROWS // 2):
        for step in range(1, COIL_DEV):
            power_copy(h, step).wait_send()


def written(images, combined, images_out, combined_out, sem):
    copies = [
        pltpu.make_async_copy(images, images_out, sem.at[0]),
        pltpu.make_async_copy(combined, combined_out, sem.at[1]),
    ]
    for copy in copies:
        copy.start()
    for copy in copies:
        copy.wait()


def on_device(kdata, coords, foot_offset, live_count, dcf_table, dcf_index, slab_owner):
    slots, coil_dev, parts, kz, samp = kdata.shape
    kd = kdata.reshape(slots, coil_dev * parts * kz, samp)
    depth = in_two(depth_table(kz))
    column = in_two(column_table(samp))
    vmem = pl.BlockSpec(memory_space=pltpu.VMEM)
    hbm = pl.BlockSpec(memory_space=pltpu.HBM)
    dma = pltpu.SemaphoreType.DMA
    images, combined = pl.pallas_call(
        body,
        out_shape=(
            jax.ShapeDtypeStruct((ROWS, coil_dev, parts, kz, samp), F32),
            jax.ShapeDtypeStruct((ROWS, kz // COIL_DEV, samp), F32),
        ),
        in_specs=[pl.BlockSpec(memory_space=pltpu.SMEM)] + [hbm] * 8,
        out_specs=(vmem, vmem),
        scratch_shapes=[
            pltpu.SMEM(slab_owner.shape, jnp.int32),
            pltpu.SMEM(dcf_table.shape, F32),
            pltpu.VMEM(coords.shape, F32),
            pltpu.VMEM(foot_offset.shape, jnp.int32),
            pltpu.VMEM(dcf_index.shape, jnp.int32),
            pltpu.VMEM(kd.shape, BF16),
            pltpu.VMEM(depth.shape, BF16),
            pltpu.VMEM(column.shape, BF16),
            pltpu.VMEM((SPOKE_DEV * BLOCK, samp), BF16),
            pltpu.VMEM((SPOKE_DEV * BLOCK * SLOTS, COLS), F32),
            pltpu.VMEM((SPOKE_DEV, BLOCK * SLOTS, 2 * COLS), BF16),
            pltpu.VMEM((SPOKE_DEV, BLOCK * SLOTS, 2 * COLS), BF16),
            pltpu.VMEM((GROUPS, 8, 128), F32),
            pltpu.VMEM((COIL_DEV, GROUPS, 8, 128), F32),
            pltpu.VMEM((GROUPS, ROWS, BAND, 256), BF16),
            pltpu.VMEM((COLS, PAIRS * 16 * PER), BF16),
            pltpu.VMEM((2, ROWS, COLS, 256), F32),
            pltpu.VMEM((ROWS, kz, samp), F32),
            pltpu.VMEM((ROWS // 2, COIL_DEV, 16, samp), BF16),
            pltpu.VMEM((ROWS // 2, COIL_DEV, 16, samp), BF16),
            dma((8,)),
            dma((GROUPS,)),
            dma((GROUPS,)),
            dma((COIL_DEV,)),
            dma((COIL_DEV,)),
            dma((2, SPOKE_DEV)),
            dma((2, SPOKE_DEV)),
            dma((ROWS // 2, COIL_DEV)),
            dma((ROWS // 2, COIL_DEV)),
        ],
        compiler_params=pltpu.CompilerParams(
            collective_id=0, has_side_effects=True, vmem_limit_bytes=24 * 2**20
        ),
    )(
        live_count,
        *(
            pltpu.with_memory_space_constraint(a, pltpu.HBM)
            for a in (slab_owner, dcf_table, coords, foot_offset, dcf_index, kd, depth, column)
        ),
    )
    return pl.pallas_call(
        written,
        out_shape=(
            jax.ShapeDtypeStruct(images.shape, F32),
            jax.ShapeDtypeStruct(combined.shape, F32),
        ),
        in_specs=[hbm] * 2,
        out_specs=(hbm, hbm),
        scratch_shapes=[dma((2,))],
        compiler_params=pltpu.CompilerParams(vmem_limit_bytes=2**20),
    )(images, combined)


def solution(mesh):
    return jax.shard_map(
        on_device,
        mesh=mesh,
        in_specs=(
            P("spoke", "coil", None, None, None),
            P("spoke", None, None),
            P("spoke", None),
            P("spoke"),
            P(),
            P("spoke", None),
            P(),
        ),
        out_specs=(P("spoke", "coil", None, None, None), P("spoke", "coil", None)),
        check_vma=False,
    )
```

time: 70.5 us -> 58.5 us (0.83)
  local copies, waits for them, and re-layouts: 7.07 us -> 0 us
  other arithmetic: 3.56 us -> 0 us
  Pallas kernels: 58.3 us -> 57.1 us
    unnamed x5 -> x0, local copies, waits for them, and re-layouts: 5.11 us -> none
    pallas_call x1, Pallas kernels: 58.3 us -> 55.7 us  [on_device(): pl.pallas_call(body, out_shape=(jax.ShapeDtypeStruct((ROWS, coil_dev, par...]
    pad x2 -> x0, local copies, waits for them, and re-layouts: 1.86 us -> none  [the longest x1 1.26 us: on_device(): table = jnp.pad(dcf_table, (0, 256 - dcf_table.shape[0])).reshape(1, 256)]
    convert_element_type x2 -> x0, other arithmetic: 1.48 us -> none  [the longest x1 0.8 us: on_device(): (wanted[:, None] == jnp.arange(samp, dtype=jnp.int32)[None, :]).astype(BF16)]
    pallas_call x0 -> x1, Pallas kernels: none -> 1.34 us  [on_device(): pl.pallas_call(written, out_shape=(jax.ShapeDtypeStruct(images.shape, F32...]
    select_n x2 -> x0, other arithmetic: 1.34 us -> none  [the longest x1 1.33 us: on_device(): jnp.where(lane >= 96, slab_owner[:, None], jnp.where(lane % 32 < BLOCK, f...]
where the time goes in v2:
time: 58.5 us; the launch traced here: 58.4 us
  Pallas kernels  57.1 us (98%)
  between operations  1.28 us (2%)
    pallas_call x1, Pallas kernels, on_device(): pl.pallas_call(body, out_shape=(jax.ShapeDtypeStruct((ROWS, coil_dev, par...  55.7 us
    pallas_call x1, Pallas kernels, on_device(): pl.pallas_call(written, out_shape=(jax.ShapeDtypeStruct(images.shape, F32...  1.34 us

profile of v2, /device:TPU:1, one launch (start us, length us, event | category | flops | bytes accessed | tf_op | source)
XLA Modules:
  0.0 58.4 jit_solution(11404082577720996078)
XLA Ops:
  1.3 55.7 %shard_map.104 = (f32[8,2,2,64,256]{4,3,2,1,0:T(8,128)S(1)}, f32[8,8,256]{2,1,0:T(8,128)S(1)}) custom-call(s32[1]{0:T(128)S(6)} %copy.11.live_ref, s32[32]{0:T(128)} %owner_hbm.1, f32[129]{0:T(256)} %table_hbm.1, f32[8,2,256]{2,1,0:T(2,128)} %coords_hbm.1, s32[8,32]{1,0:T(8,128)} %foot_hbm.1, s32[8,256]{1,0:T(8,128)} %index_hbm.1, ...), custom_call_target="tpu_custom_call" | custom-call | tf_op jit(solution)/shard_map/pallas_call | solution.py:374
  57.0 1.3 %shard_map.105 = (f32[8,2,2,64,256]{4,3,2,1,0:T(8,128)}, f32[8,8,256]{2,1,0:T(8,128)}) custom-call(f32[8,2,2,64,256]{4,3,2,1,0:T(8,128)S(1)} %get-tuple-element.4.images, f32[8,8,256]{2,1,0:T(8,128)S(1)} %get-tuple-element.5.combined), custom_call_target="tpu_custom_call" | custom-call | tf_op jit(solution)/shard_map/pallas_call | solution.py:423

commit v3 on v2

--- a/solution.py
+++ b/solution.py
@@ -23,6 +23,9 @@
 EARLY = SLOTS * (BLOCK - 2)
 COLS = 128
 GROUPS = 4
+CARRY = 4
+TILES = SPOKE_DEV // CARRY
+POWER_PARTS = ((0, 1, 2), (3,))
 PER = SPOKE_DEV // GROUPS
 BAND = 3 * 16 * PER
 F32 = jnp.float32
@@ -112,18 +115,28 @@
     lane = lax.broadcasted_iota(jnp.int32, (256, 128), 1)
     offset = lax.rem(lane, 32)
     group_of = lax.broadcasted_iota(jnp.int32, (8, 128), 1) // 32
-    half, odd = (coil + 1) // 2, lax.rem(coil, 2)
-    z_geo = lax.rem(z + odd * half + (1 - odd) * (Z_DEV - half), Z_DEV)
-    for t in range(GROUPS):
-        slab = owner_ref[x_at[t] + z_geo]
-        near = (lane < 96) & (offset < BLOCK) & (sample == slab * ROWS - REACH + offset)
-        hit = jnp.where(near | ((lane >= 96) & (sample == slab)), 1.0, 0.0).astype(BF16)
-        got = dot(geometry, hit)
-        tile = jnp.zeros((8, 128), F32)
-        for c in range(4):
-            part = got[24 * c : 24 * c + 8] + got[24 * c + 8 : 24 * c + 16] + got[24 * c + 16 : 24 * c + 24]
-            tile = jnp.where(group_of == c, part, tile)
-        geo_send[t] = tile
+    z_geo = []
+    for k in range(2):
+        r = coil + k * CARRY
+        odd = lax.rem(r, 2)
+        dz = odd * ((r + 1) // 2) + (1 - odd) * (Z_DEV - r // 2)
+        z_geo.append(lax.rem(z + dz, Z_DEV))
+
+    def geo_dest(t):
+        return x_at[t // 2] + z_geo[t % 2]
+
+    @pl.when(coil < CARRY)
+    def _():
+        for t in range(TILES):
+            slab = owner_ref[geo_dest(t)]
+            near = (lane < 96) & (offset < BLOCK) & (sample == slab * ROWS - REACH + offset)
+            hit = jnp.where(near | ((lane >= 96) & (sample == slab)), 1.0, 0.0).astype(BF16)
+            got = dot(geometry, hit)
+            tile = jnp.zeros((8, 128), F32)
+            for c in range(4):
+                part = got[24 * c : 24 * c + 8] + got[24 * c + 8 : 24 * c + 16] + got[24 * c + 16 : 24 * c + 24]
+                tile = jnp.where(group_of == c, part, tile)
+            geo_send[t] = tile
 
     row = lax.broadcasted_iota(jnp.int32, (4 * BLOCK, 256), 0)
     column = lax.broadcasted_iota(jnp.int32, (4 * BLOCK, 256), 1)
@@ -152,7 +165,7 @@
             geo.at[coil, t],
             geo_ssem.at[t],
             geo_rsem.at[t],
-            device_id=(coil, x_at[t] + z_geo),
+            device_id=(coil, geo_dest(t)),
             device_id_type=MESH,
         )
 
@@ -177,21 +190,23 @@
             device_id_type=MESH,
         )
 
-    def pass_arrival(step):
-        source = lax.rem(coil - step + COIL_DEV, COIL_DEV)
+    def pass_arrival(source):
+        step = lax.rem(coil - source + COIL_DEV, COIL_DEV)
         return pltpu.make_async_remote_copy(
             geo.at[source],
             geo.at[source],
             pass_ssem.at[step],
             pass_rsem.at[step],
-            device_id=(lax.rem(coil + step, COIL_DEV), me),
+            device_id=(coil_at[1], me),
             device_id_type=MESH,
         )
 
-    for t in range(1, GROUPS):
-        geo_copy(t).start()
-
-    @pl.when(coil != 0)
+    @pl.when(coil < CARRY)
+    def _():
+        for t in range(1, TILES):
+            geo_copy(t).start()
+
+    @pl.when((coil > 0) & (coil < CARRY))
     def _():
         geo_copy(0).start()
 
@@ -199,26 +214,42 @@
     def _():
         geo[0, 0] = geo_send[0]
 
-    for c in range(2):
-        for slot in range(1, SPOKE_DEV):
-            value_copy(c, slot, away(slot)).start()
+    for slot in range(1, SPOKE_DEV):
+        value_copy(0, slot, away(slot)).start()
+    for zt in (0, 1, 2, 3, 7, 4, 6, 5):
+        dz = lax.rem(zt - z + Z_DEV, Z_DEV)
+        back = (dz + 3) // 8
+        ahead = (dz + 7) // 8 - back
+        r = ahead * (2 * dz - 1) + back * (2 * (Z_DEV - dz))
+        for dx in (0, 1, 3, 2):
+            dest = x_at[dx] + zt
+
+            @pl.when(dest != me)
+            def _():
+                value_copy(1, dx * Z_DEV + r, dest).start()
+
 
     recv[0] = send[me]
 
-    for t in range(1, GROUPS):
-        geo_copy(t).wait_recv()
-
-    @pl.when(coil != 0)
+    @pl.when(coil < CARRY)
+    def _():
+        for t in range(1, TILES):
+            geo_copy(t).wait_recv()
+
+    @pl.when((coil > 0) & (coil < CARRY))
     def _():
         geo_copy(0).wait_recv()
 
-    @pl.loop(1, COIL_DEV)
-    def _(step):
-        pass_copy(step).start()
-
-    @pl.loop(1, COIL_DEV)
-    def _(step):
-        pass_arrival(step).wait_recv()
+    @pl.when(coil < CARRY)
+    def _():
+        for step in range(1, COIL_DEV):
+            pass_copy(step).start()
+
+    for source in range(CARRY):
+
+        @pl.when(coil != source)
+        def _():
+            pass_arrival(source).wait_recv()
 
     first_row = (owner_ref[me] * ROWS).astype(F32)
     cells = lax.broadcasted_iota(jnp.int32, (8, 256), 1).astype(F32)
@@ -227,7 +258,7 @@
     def _(slot):
         group = slot // PER
         member = lax.rem(slot, PER)
-        tile = geo[lax.rem(slot, 8), slot // 8]
+        tile = geo[lax.rem(slot, CARRY), slot // CARRY]
 
         def spread(comp, j):
             lane = comp * 32 + j
@@ -275,20 +306,22 @@
             mine = real * real + imag * imag
             power[g] = mine if c == 0 else power[g] + mine
 
-    def share(h):
-        for k in range(COIL_DEV):
-            power_send[h, k] = jnp.concatenate(
-                [power[g, 8 * k : 8 * k + 8] for g in (2 * h, 2 * h + 1)], axis=0
-            ).astype(BF16)
+    def share(part):
+        for h in POWER_PARTS[part]:
+            for k in range(COIL_DEV):
+                power_send[k, 16 * h : 16 * h + 16] = jnp.concatenate(
+                    [power[g, 8 * k : 8 * k + 8] for g in (2 * h, 2 * h + 1)], axis=0
+                ).astype(BF16)
         for step in range(1, COIL_DEV):
-            power_copy(h, step).start()
-
-    def power_copy(h, step):
+            power_copy(part, step).start()
+
+    def power_copy(part, step):
+        rows = pl.ds(16 * POWER_PARTS[part][0], 16 * len(POWER_PARTS[part]))
         return pltpu.make_async_remote_copy(
-            power_send.at[h, coil_at[step]],
-            power_recv.at[h, step],
-            pow_ssem.at[h, step],
-            pow_rsem.at[h, step],
+            power_send.at[coil_at[step], rows],
+            power_recv.at[step, rows],
+            pow_ssem.at[part, step],
+            pow_rsem.at[part, step],
             device_id=(coil_at[step], me),
             device_id_type=MESH,
         )
@@ -307,7 +340,7 @@
     for h in range(ROWS // 2 - 1):
         transform(0, h)
         transform(1, h)
-        share(h)
+    share(0)
     for q in range(GROUPS):
         arrived(1, q)
         for c in range(2):
@@ -317,18 +350,19 @@
                 grid[c, g] = grid[c, g] + dot(got, weights[q, g, BAND - 16 * PER :])
     for c in range(2):
         transform(c, ROWS // 2 - 1)
-    share(ROWS // 2 - 1)
-
-    for h in range(ROWS // 2):
-        power_recv[h, 0] = power_send[h, coil]
+    share(1)
+
+    for part, lines in enumerate(POWER_PARTS):
         for step in range(1, COIL_DEV):
-            power_copy(h, step).wait_recv()
-        total = power_recv[h, 0].astype(F32)
-        for k in range(1, COIL_DEV):
-            total = total + power_recv[h, k].astype(F32)
-        combined = jnp.sqrt(total)
-        combined_ref[2 * h] = combined[:8]
-        combined_ref[2 * h + 1] = combined[8:]
+            power_copy(part, step).wait_recv()
+        for h in lines:
+            rows = pl.ds(16 * h, 16)
+            total = power_send[coil, rows].astype(F32)
+            for k in range(1, COIL_DEV):
+                total = total + power_recv[k, rows].astype(F32)
+            combined = jnp.sqrt(total)
+            combined_ref[2 * h] = combined[:8]
+            combined_ref[2 * h + 1] = combined[8:]
 
     for c in range(2):
 
@@ -336,20 +370,20 @@
         def _(slot):
             value_copy(c, slot, x_at[1]).wait_send()
 
-    for t in range(1, GROUPS):
-        geo_copy(t).wait_send()
-
-    @pl.when(coil != 0)
+    @pl.when(coil < CARRY)
+    def _():
+        for t in range(1, TILES):
+            geo_copy(t).wait_send()
+        for step in range(1, COIL_DEV):
+            pass_copy(step).wait_send()
+
+    @pl.when((coil > 0) & (coil < CARRY))
     def _():
         geo_copy(0).wait_send()
 
-    @pl.loop(1, COIL_DEV)
-    def _(step):
-        pass_copy(step).wait_send()
-
-    for h in range(ROWS // 2):
+    for part in range(len(POWER_PARTS)):
         for step in range(1, COIL_DEV):
-            power_copy(h, step).wait_send()
+            power_copy(part, step).wait_send()
 
 
 def written(images, combined, images_out, combined_out, sem):
@@ -392,23 +426,23 @@
             pltpu.VMEM((SPOKE_DEV * BLOCK * SLOTS, COLS), F32),
             pltpu.VMEM((SPOKE_DEV, BLOCK * SLOTS, 2 * COLS), BF16),
             pltpu.VMEM((SPOKE_DEV, BLOCK * SLOTS, 2 * COLS), BF16),
-            pltpu.VMEM((GROUPS, 8, 128), F32),
-            pltpu.VMEM((COIL_DEV, GROUPS, 8, 128), F32),
+            pltpu.VMEM((TILES, 8, 128), F32),
+            pltpu.VMEM((CARRY, TILES, 8, 128), F32),
             pltpu.VMEM((GROUPS, ROWS, BAND, 256), BF16),
             pltpu.VMEM((COLS, PAIRS * 16 * PER), BF16),
             pltpu.VMEM((2, ROWS, COLS, 256), F32),
             pltpu.VMEM((ROWS, kz, samp), F32),
-            pltpu.VMEM((ROWS // 2, COIL_DEV, 16, samp), BF16),
-            pltpu.VMEM((ROWS // 2, COIL_DEV, 16, samp), BF16),
+            pltpu.VMEM((COIL_DEV, ROWS * 8, samp), BF16),
+            pltpu.VMEM((COIL_DEV, ROWS * 8, samp), BF16),
             dma((8,)),
-            dma((GROUPS,)),
-            dma((GROUPS,)),
+            dma((TILES,)),
+            dma((TILES,)),
             dma((COIL_DEV,)),
             dma((COIL_DEV,)),
             dma((2, SPOKE_DEV)),
             dma((2, SPOKE_DEV)),
-            dma((ROWS // 2, COIL_DEV)),
-            dma((ROWS // 2, COIL_DEV)),
+            dma((len(POWER_PARTS), COIL_DEV)),
+            dma((len(POWER_PARTS), COIL_DEV)),
         ],
         compiler_params=pltpu.CompilerParams(
             collective_id=0, has_side_effects=True, vmem_limit_bytes=24 * 2**20

time: 58.5 us -> 57 us (0.974)
  Pallas kernels: 57.1 us -> 55.7 us
    pallas_call x1, Pallas kernels: 55.7 us -> 54.3 us  [on_device(): pl.pallas_call(body, out_shape=(jax.ShapeDtypeStruct((ROWS, coil_dev, par...]
where the time goes in v3:
time: 57 us; the launch traced here: 56.9 us
  Pallas kernels  55.7 us (98%)
  between operations  1.28 us (2%)
    pallas_call x1, Pallas kernels, on_device(): pl.pallas_call(body, out_shape=(jax.ShapeDtypeStruct((ROWS, coil_dev, par...  54.3 us
    pallas_call x1, Pallas kernels, on_device(): pl.pallas_call(written, out_shape=(jax.ShapeDtypeStruct(images.shape, F32...  1.34 us

profile of v3, /device:TPU:1, one launch (start us, length us, event | category | flops | bytes accessed | tf_op | source)
XLA Modules:
  0.0 56.9 jit_solution(14498467039726195254)
XLA Ops:
  1.3 54.3 %shard_map.104 = (f32[8,2,2,64,256]{4,3,2,1,0:T(8,128)S(1)}, f32[8,8,256]{2,1,0:T(8,128)S(1)}) custom-call(s32[1]{0:T(128)S(6)} %copy.11.live_ref, s32[32]{0:T(128)} %owner_hbm.1, f32[129]{0:T(256)} %table_hbm.1, f32[8,2,256]{2,1,0:T(2,128)} %coords_hbm.1, s32[8,32]{1,0:T(8,128)} %foot_hbm.1, s32[8,256]{1,0:T(8,128)} %index_hbm.1, ...), custom_call_target="tpu_custom_call" | custom-call | tf_op jit(solution)/shard_map/pallas_call | solution.py:408
  55.6 1.3 %shard_map.105 = (f32[8,2,2,64,256]{4,3,2,1,0:T(8,128)}, f32[8,8,256]{2,1,0:T(8,128)}) custom-call(f32[8,2,2,64,256]{4,3,2,1,0:T(8,128)S(1)} %get-tuple-element.4.images, f32[8,8,256]{2,1,0:T(8,128)S(1)} %get-tuple-element.5.combined), custom_call_target="tpu_custom_call" | custom-call | tf_op jit(solution)/shard_map/pallas_call | solution.py:457

commit v4 on v3

--- a/solution.py
+++ b/solution.py
@@ -352,6 +352,23 @@
         transform(c, ROWS // 2 - 1)
     share(1)
 
+    for c in range(2):
+
+        @pl.loop(1, SPOKE_DEV)
+        def _(slot):
+            value_copy(c, slot, x_at[1]).wait_send()
+
+    @pl.when(coil < CARRY)
+    def _():
+        for t in range(1, TILES):
+            geo_copy(t).wait_send()
+        for step in range(1, COIL_DEV):
+            pass_copy(step).wait_send()
+
+    @pl.when((coil > 0) & (coil < CARRY))
+    def _():
+        geo_copy(0).wait_send()
+
     for part, lines in enumerate(POWER_PARTS):
         for step in range(1, COIL_DEV):
             power_copy(part, step).wait_recv()
@@ -363,23 +380,6 @@
             combined = jnp.sqrt(total)
             combined_ref[2 * h] = combined[:8]
             combined_ref[2 * h + 1] = combined[8:]
-
-    for c in range(2):
-
-        @pl.loop(1, SPOKE_DEV)
-        def _(slot):
-            value_copy(c, slot, x_at[1]).wait_send()
-
-    @pl.when(coil < CARRY)
-    def _():
-        for t in range(1, TILES):
-            geo_copy(t).wait_send()
-        for step in range(1, COIL_DEV):
-            pass_copy(step).wait_send()
-
-    @pl.when((coil > 0) & (coil < CARRY))
-    def _():
-        geo_copy(0).wait_send()
 
     for part in range(len(POWER_PARTS)):
         for step in range(1, COIL_DEV):

time: 57 us -> 56.6 us (level)
  no operation moved by 1% of the time
where the time goes in v4:
time: 56.6 us; the launch traced here: 56.5 us
  Pallas kernels  55.2 us (98%)
  between operations  1.28 us (2%)
    pallas_call x1, Pallas kernels, on_device(): pl.pallas_call(body, out_shape=(jax.ShapeDtypeStruct((ROWS, coil_dev, par...  53.9 us
    pallas_call x1, Pallas kernels, on_device(): pl.pallas_call(written, out_shape=(jax.ShapeDtypeStruct(images.shape, F32...  1.34 us

profile of v4, /device:TPU:1, one launch (start us, length us, event | category | flops | bytes accessed | tf_op | source)
XLA Modules:
  0.0 56.5 jit_solution(4006706060922899666)
XLA Ops:
  1.3 53.9 %shard_map.104 = (f32[8,2,2,64,256]{4,3,2,1,0:T(8,128)S(1)}, f32[8,8,256]{2,1,0:T(8,128)S(1)}) custom-call(s32[1]{0:T(128)S(6)} %copy.11.live_ref, s32[32]{0:T(128)} %owner_hbm.1, f32[129]{0:T(256)} %table_hbm.1, f32[8,2,256]{2,1,0:T(2,128)} %coords_hbm.1, s32[8,32]{1,0:T(8,128)} %foot_hbm.1, s32[8,256]{1,0:T(8,128)} %index_hbm.1, ...), custom_call_target="tpu_custom_call" | custom-call | tf_op jit(solution)/shard_map/pallas_call | solution.py:408
  55.1 1.3 %shard_map.105 = (f32[8,2,2,64,256]{4,3,2,1,0:T(8,128)}, f32[8,8,256]{2,1,0:T(8,128)}) custom-call(f32[8,2,2,64,256]{4,3,2,1,0:T(8,128)S(1)} %get-tuple-element.4.images, f32[8,8,256]{2,1,0:T(8,128)S(1)} %get-tuple-element.5.combined), custom_call_target="tpu_custom_call" | custom-call | tf_op jit(solution)/shard_map/pallas_call | solution.py:457
